TPU v7x, 32 devices: a whole 2x2x4 slice. The times are simulated.
32 devices in a mesh: shard: 8 (over z, x), rep: 4 (over y, core).
Axes of the slice: x: 2, y: 2, z: 4, core: 2. Of those that a mesh axis runs over, the one named last changes fastest.
Arguments:
- lender_block: int32 [96, 8], P(('shard', 'rep')), may hold values from 0 to 255, as said below
- confidence: bfloat16 [96, 8, 256, 256], P(('shard', 'rep')), may hold values from 0 to 80, as said below
- lender_factors: bfloat16 [65536, 128], P('shard'), may hold values from -4 to 4
Outputs:
- borrower_factors: float32 [24576, 128], P(('shard', 'rep'))
- lender_rhs: float32 [65536, 128], P('shard')
Inputs may be any that keep to these rules, and one draw needn't show every extreme that they name: `lender_block`: within one device's 3 borrower blocks, at most 6 of the 3 x 8 entries name blocks of any one owner (block // 32), and on every device some owner is named exactly 6 times. `confidence`: about half the entries are zero; the others are positive.
All inputs are finite; a program needn't handle non-finite values.
Results may differ from a plain program's by a relative error of at most 0.0047.
Values may be sent and summed in bfloat16 or wider, within the bound.
A program may use at most 128 MiB of HBM per device.

v0:
```python
import jax
import jax.numpy as jnp
from jax import lax
from jax.sharding import PartitionSpec as P

CG_STEPS = 3
HIGH = lax.Precision.HIGHEST


def apply_system(direction, confidence, fetched, gram):
    low = direction.astype(jnp.bfloat16)
    scores = jnp.einsum("btr,bklr->bktl", low, fetched, preferred_element_type=jnp.float32)
    weighted = (confidence.astype(jnp.float32) * scores).astype(jnp.bfloat16)
    back = jnp.einsum("bktl,bklr->btr", weighted, fetched, preferred_element_type=jnp.float32)
    width = direction.shape[-1]
    global_part = jnp.dot(
        direction.reshape(-1, width), gram, precision=HIGH, preferred_element_type=jnp.float32
    )
    return global_part.reshape(direction.shape) + 0.1 * direction + back


def per_device(lender_block, confidence, lender_factors):
    shards = lax.axis_size("shard")
    blocks, lists = lender_block.shape
    tile = confidence.shape[2]
    rank = lender_factors.shape[1]
    owned = lender_factors.shape[0] // tile
    entries = blocks * lists
    slots = (2 * entries + shards - 1) // shards
    local_gram = lax.dot_general(
        lender_factors, lender_factors, (((0,), (0,)), ((), ())), preferred_element_type=jnp.float32
    )
    gram = lax.psum(local_gram, "shard")
    flat = lender_block.reshape(entries)
    owner = flat // owned
    within = flat - owner * owned
    member = (owner[:, None] == jnp.arange(shards, dtype=jnp.int32)[None, :]).astype(jnp.int32)
    position = jnp.sum(jnp.cumsum(member, axis=0) * member, axis=1) - 1
    slot_index = owner * slots + position
    requests = (
        jnp.zeros((shards * slots,), jnp.int32).at[slot_index].set(within).reshape(shards, slots)
    )
    table = lender_factors.reshape(owned, tile, rank)
    incoming = lax.all_to_all(requests, "shard", split_axis=0, concat_axis=0, tiled=True)
    replies = lax.all_to_all(table[incoming], "shard", split_axis=0, concat_axis=0, tiled=True)
    fetched = replies.reshape(shards * slots, tile, rank)[slot_index].reshape(
        blocks, lists, tile, rank
    )
    rhs = jnp.einsum("bktl,bklr->btr", confidence, fetched, preferred_element_type=jnp.float32)
    solution = jnp.zeros_like(rhs)
    resid = rhs
    direction = rhs
    norm_now = jnp.sum(resid * resid, axis=2, keepdims=True)
    for count in range(CG_STEPS):
        image = apply_system(direction, confidence, fetched, gram)
        alpha = norm_now / (jnp.sum(direction * image, axis=2, keepdims=True) + 1e-06)
        solution = solution + alpha * direction
        resid = resid - alpha * image
        norm_next = jnp.sum(resid * resid, axis=2, keepdims=True)
        direction = resid + norm_next / (norm_now + 1e-06) * direction
        norm_now = norm_next
    solved = solution.astype(jnp.bfloat16)
    partial_rhs = jnp.einsum(
        "bktl,btr->bklr", confidence, solved, preferred_element_type=jnp.float32
    )
    outgoing = (
        jnp.zeros((shards * slots, tile, rank), jnp.float32)
        .at[slot_index]
        .set(partial_rhs.reshape(entries, tile, rank))
    )
    returned = lax.all_to_all(
        outgoing.reshape(shards, slots, tile, rank),
        "shard",
        split_axis=0,
        concat_axis=0,
        tiled=True,
    )
    selector = (
        incoming.reshape(-1)[None, :] == jnp.arange(owned, dtype=jnp.int32)[:, None]
    ).astype(jnp.float32)
    owner_sum = jnp.dot(
        selector,
        returned.reshape(shards * slots, tile * rank),
        precision=HIGH,
        preferred_element_type=jnp.float32,
    )
    total = lax.psum(owner_sum, "rep")
    lenders_all = owned * tile * shards
    lender_rhs = total.reshape(owned * tile, rank) / lenders_all
    return (solution.reshape(blocks * tile, rank), lender_rhs)


def solution(mesh):
    in_specs = (P(("shard", "rep"), None), P(("shard", "rep"), None, None, None), P("shard", None))
    out_specs = (P(("shard", "rep"), None), P("shard", None))
    return jax.shard_map(
        per_device, mesh=mesh, in_specs=in_specs, out_specs=out_specs, check_vma=False
    )
```

profile of v0, /device:TPU:0, one launch (start us, length us, event | category | flops | bytes accessed | tf_op | source)
XLA Modules:
  0.0 416.2 jit_solution(9014133852448018927)
XLA Ops:
  7.2 0.9 reshape.224
  8.1 0.8 reshape.223
  9.2 0.6 scatter_custom_fusion
  9.9 13.6 %all_to_all.22 = s32[8,1,6]{2,1,0:T(1,128)S(1)} all-to-all(s32[8,1,6]{2,1,0:T(1,128)S(1)} %bitcast.112), channel_id=1, replica_groups=mesh['shard'=8,'rep'=4] {'shard'}, dimensions={0} | all-to-all | bytes 384 | tf_op jit(solution)/shard_map/all_to_all | solution.py:44
  23.8 2.7 gather_fusion
  26.5 4.4 %all-to-all-start.1 = ((bf16[8,6,256,128]{3,2,1,0:T(8,128)(2,1)}), bf16[8,6,256,128]{3,2,1,0:T(8,128)(2,1)}, u32[]{:S(2)}, u32[]{:S(2)}) async-start(bf16[8,6,256,128]{3,2,1,0:T(8,128)(2,1)} %bitcast.106), calls=%async_computation.1 | async-start | bytes 6291456 | tf_op jit(solution)/shard_map/all_to_all | solution.py:45
  31.0 1.4 fusion.55
  32.4 4.7 %copy.37 = bf16[3,8,256,256]{2,3,1,0:T(8,128)(2,1)} copy(bf16[3,8,256,256]{3,2,1,0:T(8,128)(2,1)} %param.4) | data formatting | bytes 6291456 | tf_op args[1]
  37.1 64.9 %all-to-all-done.1 = bf16[8,6,256,128]{3,2,1,0:T(8,128)(2,1)} async-done(((bf16[8,6,256,128]{3,2,1,0:T(8,128)(2,1)}), bf16[8,6,256,128]{3,2,1,0:T(8,128)(2,1)}, u32[]{:S(2)}, u32[]{:S(2)}) %all-to-all-start.1) | async-done | bytes 3145760 | tf_op jit(solution)/shard_map/all_to_all | solution.py:45
  102.0 3.8 gather_fusion.1
  105.8 3.5 convolution_bitcast_fusion
  109.4 4.3 %fusion.18 = f32[3,256,128]{1,2,0:T(8,128)S(1)} fusion(bf16[3,8,256,128]{3,2,1,0:T(8,128)(2,1)} %bitcast.108, bf16[3,8,256,256]{2,3,1,0:T(8,128)(2,1)} %copy.37, f32[3,256,128]{1,2,0:T(8,128)S(1)} %convolution_bitcast_fusion), kind=kOutput, calls=%fused_computation.20 | convolution fusion | flops 810123264 | bytes 5505024 | tf_op jit(solution)/shard_map/bktl,bklr->btr/dot_general | solution.py:14
  113.7 13.5 %all-reduce.3.cloned.1.call-done = f32[128,128]{1,0:T(8,128)} async-done(((f32[128,128]{1,0:T(8,128)}), f32[128,128]{1,0:T(8,128)}) %all-reduce.3.cloned.1.call-update) | async-done | bytes 65552 | tf_op jit(solution)/shard_map/psum | solution.py:33
  127.2 1.4 multiply_reduce_fusion.3
  128.8 5.1 %fusion.21 = f32[3,256,128]{1,2,0:T(8,128)} fusion(bf16[3,8,256,128]{3,2,1,0:T(8,128)(2,1)} %bitcast.109, bf16[3,8,256,256]{2,3,1,0:T(8,128)(2,1)} %copy.37, f32[3,256,128]{1,2,0:T(8,128)S(1)} %multiply_add_fusion.2), kind=kOutput, calls=%fused_computation.21 | convolution fusion | flops 810123264 | bytes 5505024 | tf_op jit(solution)/shard_map/bktl,bklr->btr/dot_general | solution.py:14
  133.8 1.6 multiply_reduce_fusion.1
  135.5 0.8 multiply_add_fusion.1
  136.3 5.2 %fusion.24 = f32[3,256,128]{1,2,0:T(8,128)} fusion(bf16[3,8,256,128]{3,2,1,0:T(8,128)(2,1)} %bitcast.110, bf16[3,8,256,256]{2,3,1,0:T(8,128)(2,1)} %copy.37, f32[3,256,128]{1,2,0:T(8,128)} %multiply_add_fusion.1), kind=kOutput, calls=%fused_computation.22 | convolution fusion | flops 810123264 | bytes 5505024 | tf_op jit(solution)/shard_map/bktl,bklr->btr/dot_general | solution.py:14
  141.5 1.6 fusion.31
  143.1 1.1 multiply_add_fusion
  144.2 4.1 fusion.38
  148.3 3.6 copy.52
  151.9 3.4 broadcast_in_dim.5
  155.3 7.9 %scatter_fusion = f32[48,256,128]{2,1,0:T(8,128)} fusion(f32[48,256,128]{2,1,0:T(8,128)} %broadcast_in_dim.5, s32[24]{0:T(128)S(1)} %fusion.52, f32[24,256,128]{2,1,0:T(8,128)} %copy.52), kind=kCustom, calls=%fused_computation.3 | custom fusion | bytes 9437280 | tf_op jit(solution)/shard_map/scatter | solution.py:69
  163.3 4.8 %all-to-all-start.2 = ((f32[8,6,256,128]{3,2,1,0:T(8,128)}), f32[8,6,256,128]{3,2,1,0:T(8,128)}, u32[]{:S(2)}, u32[]{:S(2)}) async-start(f32[8,6,256,128]{3,2,1,0:T(8,128)} %bitcast.104), calls=%async_computation.2 | async-start | bytes 12582912 | tf_op jit(solution)/shard_map/all_to_all | solution.py:71
  168.8 0.7 reduce.3
  169.5 135.1 %all-to-all-done.2 = f32[8,6,256,128]{3,2,1,0:T(8,128)} async-done(((f32[8,6,256,128]{3,2,1,0:T(8,128)}), f32[8,6,256,128]{3,2,1,0:T(8,128)}, u32[]{:S(2)}, u32[]{:S(2)}) %all-to-all-start.2) | async-done | bytes 6291488 | tf_op jit(solution)/shard_map/all_to_all | solution.py:71
  304.6 10.8 %fusion.3 = f32[32,32768]{1,0:T(8,128)} fusion(f32[6,8,256,128]{3,2,1,0:T(8,128)} %bitcast.40, s32[48]{0:T(128)S(1)} %eq.31), kind=kOutput, calls=%fused_computation.10 | convolution fusion | flops 603981312 | bytes 10485952 | tf_op jit(solution)/shard_map/dot_general | solution.py:81
  315.4 0.9 copy.51
  316.3 83.7 %all-reduce.5.cloned.1.call-done = f32[32,32768]{1,0:T(8,128)} async-done(((f32[32,32768]{1,0:T(8,128)}), f32[32,32768]{1,0:T(8,128)}) %all-reduce.5.cloned.1.call-update) | async-done | bytes 4194320 | tf_op jit(solution)/shard_map/psum | solution.py:87
  400.0 4.4 %broadcast_multiply_fusion = f32[32,32768]{1,0:T(8,128)} fusion(f32[32,32768]{1,0:T(8,128)} %all-reduce.5.cloned.1.call-done), kind=kLoop, calls=%fused_computation.19 | loop fusion | flops 1048576 | bytes 8388608 | tf_op jit(solution)/shard_map/div | solution.py:89
  404.5 4.9 %div.83 = f32[8192,128]{1,0:T(8,128)} reshape(f32[32,32768]{1,0:T(8,128)} %broadcast_multiply_fusion) | data formatting | bytes 8388608 | tf_op jit(solution)/shard_map/div | solution.py:89
  (32 shorter events, 1.8 us)
Async XLA Ops:
  7.2 16.6 %copy-start = (bf16[8192,128]{1,0:T(8,128)(2,1)S(1)}, bf16[8192,128]{1,0:T(8,128)(2,1)}, u32[]{:S(2)}) copy-start(bf16[8192,128]{1,0:T(8,128)(2,1)} %param.5) | copy-start | bytes 6291460
  26.5 75.5 %all-to-all-start.1 = ((bf16[8,6,256,128]{3,2,1,0:T(8,128)(2,1)}), bf16[8,6,256,128]{3,2,1,0:T(8,128)(2,1)}, u32[]{:S(2)}, u32[]{:S(2)}) async-start(bf16[8,6,256,128]{3,2,1,0:T(8,128)(2,1)} %bitcast.106), calls=%async_computation.1 | async-start | bytes 6291456 | tf_op jit(solution)/shard_map/all_to_all | solution.py:45
  30.9 96.2 %all-reduce.3.cloned.1.call-start = ((), (), s32[]{:S(2)}) async-start(), calls=%async_computation.3 | async-start | bytes 131072 | tf_op jit(solution)/shard_map/psum | solution.py:33
  128.7 5.1 %copy-start.2 = (f32[128,128]{1,0:T(8,128)S(1)}, f32[128,128]{1,0:T(8,128)}, u32[]{:S(2)}) copy-start(f32[128,128]{1,0:T(8,128)} %all-reduce.3.cloned.1.call-done) | copy-start | bytes 196612
  136.3 5.2 %copy-start.1 = (f32[3,256,128]{1,2,0:T(8,128)S(1)}, f32[3,256,128]{1,2,0:T(8,128)}, u32[]{:S(2)}) copy-start(f32[3,256,128]{1,2,0:T(8,128)} %multiply_add_fusion.1) | copy-start | bytes 1179652
  163.3 141.3 %all-to-all-start.2 = ((f32[8,6,256,128]{3,2,1,0:T(8,128)}), f32[8,6,256,128]{3,2,1,0:T(8,128)}, u32[]{:S(2)}, u32[]{:S(2)}) async-start(f32[8,6,256,128]{3,2,1,0:T(8,128)} %bitcast.104), calls=%async_computation.2 | async-start | bytes 12582912 | tf_op jit(solution)/shard_map/all_to_all | solution.py:71
  168.0 232.0 %all-reduce.5.cloned.1.call-start = ((), (), s32[]{:S(2)}) async-start(), calls=%async_computation.4 | async-start | bytes 8388608 | tf_op jit(solution)/shard_map/psum | solution.py:87
Sparse Core Ops, SparseCore 0:
  35.7 91.3 all-reduce.2
  315.5 84.4 all-reduce.4
where the time goes:
time: 417 us; the launch traced here: 416 us
  waiting for transfers between devices  297 us (71%)
  matrix products  39 us (9%)
  local copies, waits for them, and re-layouts  35.2 us (8%)
  between operations  14.2 us (3%)
  blocking collectives  13.6 us (3%)
  starting transfers between devices  9.46 us (2%)
  other arithmetic  7.59 us (2%)
    all_to_all x1, waiting for transfers between devices, per_device(): lax.all_to_all(outgoing.reshape(shards, slots, tile, rank), 'shard', spli...  135 us
    psum x1, waiting for transfers between devices, per_device(): total = lax.psum(owner_sum, 'rep')  83.7 us
    all_to_all x1, waiting for transfers between devices, per_device(): lax.all_to_all(table[incoming], 'shard', split_axis=0, concat_axis=0, til...  64.9 us
    dot_general x3, matrix products, apply_system(): jnp.einsum('bktl,bklr->btr', weighted, fetched, preferred_element_type=jn...  14.5 us
    all_to_all x1, blocking collectives, per_device(): lax.all_to_all(requests, 'shard', split_axis=0, concat_axis=0, tiled=True)  13.6 us
    psum x1, waiting for transfers between devices, per_device(): gram = lax.psum(local_gram, 'shard')  13.5 us
    dot_general x1, matrix products, per_device(): jnp.dot(selector, returned.reshape(shards * slots, tile * rank), precisio...  10.8 us
  transfers between devices with their start and end apart: 4, of which 4 were waited for; matrix products, arithmetic and copies ran while one was open for 5% of the time, Pallas kernels for 0%

commit v1 on v0

--- a/solution.py
+++ b/solution.py
@@ -30,7 +30,10 @@
     local_gram = lax.dot_general(
         lender_factors, lender_factors, (((0,), (0,)), ((), ())), preferred_element_type=jnp.float32
     )
-    gram = lax.psum(local_gram, "shard")
+    size, gram = (lax.axis_size("shard"), local_gram)
+    for far in [1 << k for k in range(size.bit_length() - 1)]:
+        pairs = [(i, i ^ far) for i in range(size)]
+        gram = gram + lax.ppermute(gram, "shard", pairs)
     flat = lender_block.reshape(entries)
     owner = flat // owned
     within = flat - owner * owned

time: 417 us -> 403 us (0.966)
  waiting for transfers between devices: 297 us -> 278 us
  starting transfers between devices: 9.46 us -> 16.2 us
    all_to_all x1, waiting for transfers between devices: 64.9 us -> 16 us  [per_device(): lax.all_to_all(table[incoming], 'shard', split_axis=0, concat_axis=0, til...]
    ppermute x0 -> x3, waiting for transfers between devices: none -> 43.4 us  [per_device(): gram = gram + lax.ppermute(gram, 'shard', pairs)]
    psum x1 -> x0, waiting for transfers between devices: 13.5 us -> none  [per_device(): gram = lax.psum(local_gram, 'shard')]
    ppermute x0 -> x3, starting transfers between devices: none -> 6.77 us  [per_device(): gram = gram + lax.ppermute(gram, 'shard', pairs)]
  transfers between devices with their start and end apart: 4 -> 6, of which waited for: 4 -> 5; matrix products, arithmetic and copies ran while one was open for 5% -> 5% of each run, Pallas kernels for 0% -> 0%
where the time goes in v1:
time: 403 us
  waiting for transfers between devices  278 us (69%)
  matrix products  37.5 us (9%)
  local copies, waits for them, and re-layouts  35.2 us (9%)
  starting transfers between devices  16.2 us (4%)
  between operations  14.2 us (4%)
  blocking collectives  13.6 us (3%)
  other arithmetic  7.61 us (2%)
    all_to_all x1, waiting for transfers between devices, per_device(): lax.all_to_all(outgoing.reshape(shards, slots, tile, rank), 'shard', spli...  135 us
    psum x1, waiting for transfers between devices, per_device(): total = lax.psum(owner_sum, 'rep')  83.9 us
    ppermute x3, waiting for transfers between devices, per_device(): gram = gram + lax.ppermute(gram, 'shard', pairs)  43.4 us
    all_to_all x1, waiting for transfers between devices, per_device(): lax.all_to_all(table[incoming], 'shard', split_axis=0, concat_axis=0, til...  16 us
    dot_general x3, matrix products, apply_system(): jnp.einsum('bktl,bklr->btr', weighted, fetched, preferred_element_type=jn...  14.5 us
    all_to_all x1, blocking collectives, per_device(): lax.all_to_all(requests, 'shard', split_axis=0, concat_axis=0, tiled=True)  13.6 us
    dot_general x1, matrix products, per_device(): jnp.dot(selector, returned.reshape(shards * slots, tile * rank), precisio...  10.8 us
  transfers between devices with their start and end apart: 6, of which 5 were waited for; matrix products, arithmetic and copies ran while one was open for 5% of the time, Pallas kernels for 0%

profile of v1, /device:TPU:0, one launch (start us, length us, event | category | flops | bytes accessed | tf_op | source)
XLA Modules:
  0.0 402.7 jit_solution(14195204897366665761)
XLA Ops:
  7.2 0.9 reshape.224
  8.1 0.8 reshape.223
  9.9 13.6 %all_to_all.22 = s32[8,1,6]{2,1,0:T(1,128)S(1)} all-to-all(s32[8,1,6]{2,1,0:T(1,128)S(1)} %bitcast.112), channel_id=1, replica_groups=mesh['shard'=8,'rep'=4] {'shard'}, dimensions={0} | all-to-all | bytes 384 | tf_op jit(solution)/shard_map/all_to_all | solution.py:47
  23.8 2.7 gather_fusion
  26.5 4.4 %all-to-all-start.1 = ((bf16[8,6,256,128]{3,2,1,0:T(8,128)(2,1)}), bf16[8,6,256,128]{3,2,1,0:T(8,128)(2,1)}, u32[]{:S(2)}, u32[]{:S(2)}) async-start(bf16[8,6,256,128]{3,2,1,0:T(8,128)(2,1)} %bitcast.106), calls=%async_computation.1 | async-start | bytes 6291456 | tf_op jit(solution)/shard_map/all_to_all | solution.py:48
  31.7 2.0 collective-permute-start
  33.6 4.7 %copy.37 = bf16[3,8,256,256]{2,3,1,0:T(8,128)(2,1)} copy(bf16[3,8,256,256]{3,2,1,0:T(8,128)(2,1)} %param.4) | data formatting | bytes 6291456 | tf_op args[1]
  38.3 19.2 %collective-permute-done = f32[128,128]{1,0:T(8,128)S(1)} collective-permute-done((f32[128,128]{1,0:T(8,128)S(1)}, f32[128,128]{1,0:T(8,128)S(1)}, u32[]{:S(2)}, u32[]{:S(2)}) %collective-permute-start) | collective-permute-done | bytes 65568 | tf_op jit(solution)/shard_map/ppermute | solution.py:36
  57.5 0.8 collective-permute-start.1
  58.3 24.2 %collective-permute-done.1 = f32[128,128]{1,0:T(8,128)S(1)} collective-permute-done((f32[128,128]{1,0:T(8,128)S(1)}, f32[128,128]{1,0:T(8,128)S(1)}, u32[]{:S(2)}, u32[]{:S(2)}) %collective-permute-start.1) | collective-permute-done | bytes 65568 | tf_op jit(solution)/shard_map/ppermute | solution.py:36
  82.6 4.0 %collective-permute-start.2 = (f32[128,128]{1,0:T(8,128)S(1)}, f32[128,128]{1,0:T(8,128)S(1)}, u32[]{:S(2)}, u32[]{:S(2)}) collective-permute-start(f32[128,128]{1,0:T(8,128)S(1)} %add.141), channel_id=1, source_target_pairs={{0,16},{4,20},{8,24},{12,28},{16,0},{20,4},{24,8},{28,12},{1,17},{... | collective-permute-start | bytes 196616 | tf_op jit(solution)/shard_map/ppermute | solution.py:36
  86.6 16.0 %all-to-all-done.1 = bf16[8,6,256,128]{3,2,1,0:T(8,128)(2,1)} async-done(((bf16[8,6,256,128]{3,2,1,0:T(8,128)(2,1)}), bf16[8,6,256,128]{3,2,1,0:T(8,128)(2,1)}, u32[]{:S(2)}, u32[]{:S(2)}) %all-to-all-start.1) | async-done | bytes 3145760 | tf_op jit(solution)/shard_map/all_to_all | solution.py:48
  102.6 3.8 gather_fusion.1
  106.4 3.5 convolution_bitcast_fusion
  110.0 4.3 %fusion.18 = f32[3,256,128]{1,2,0:T(8,128)S(1)} fusion(bf16[3,8,256,128]{3,2,1,0:T(8,128)(2,1)} %bitcast.108, bf16[3,8,256,256]{2,3,1,0:T(8,128)(2,1)} %copy.37, f32[3,256,128]{1,2,0:T(8,128)S(1)} %convolution_bitcast_fusion), kind=kOutput, calls=%fused_computation.20 | convolution fusion | flops 810123264 | bytes 5505024 | tf_op jit(solution)/shard_map/bktl,bklr->btr/dot_general | solution.py:14
  115.0 5.0 %fusion.21 = f32[3,256,128]{1,2,0:T(8,128)} fusion(bf16[3,8,256,128]{3,2,1,0:T(8,128)(2,1)} %bitcast.109, bf16[3,8,256,256]{2,3,1,0:T(8,128)(2,1)} %copy.37, f32[3,256,128]{1,2,0:T(8,128)S(1)} %multiply_add_fusion.2), kind=kOutput, calls=%fused_computation.21 | convolution fusion | flops 810123264 | bytes 5505024 | tf_op jit(solution)/shard_map/bktl,bklr->btr/dot_general | solution.py:14
  120.1 1.6 multiply_reduce_fusion.1
  121.7 0.8 multiply_add_fusion.1
  122.6 5.2 %fusion.24 = f32[3,256,128]{1,2,0:T(8,128)} fusion(bf16[3,8,256,128]{3,2,1,0:T(8,128)(2,1)} %bitcast.110, bf16[3,8,256,256]{2,3,1,0:T(8,128)(2,1)} %copy.37, f32[3,256,128]{1,2,0:T(8,128)} %multiply_add_fusion.1), kind=kOutput, calls=%fused_computation.22 | convolution fusion | flops 810123264 | bytes 5505024 | tf_op jit(solution)/shard_map/bktl,bklr->btr/dot_general | solution.py:14
  127.8 1.6 fusion.31
  129.3 1.1 multiply_add_fusion
  130.4 4.1 %fusion.38 = f32[3,128,8,256]{3,1,2,0:T(8,128)} fusion(bf16[3,8,256,256]{3,2,1,0:T(8,128)(2,1)} %param.4, f32[3,256,128]{1,2,0:T(8,128)S(1)} %multiply_add_fusion), kind=kOutput, calls=%fused_computation.45 | convolution fusion | flops 402751488 | bytes 6684672 | tf_op jit(solution)/shard_map/bktl,btr->bklr/dot_general | solution.py:66
  134.5 3.6 copy.52
  138.1 3.4 broadcast_in_dim.5
  141.5 7.9 %scatter_fusion = f32[48,256,128]{2,1,0:T(8,128)} fusion(f32[48,256,128]{2,1,0:T(8,128)} %broadcast_in_dim.5, s32[24]{0:T(128)S(1)} %fusion.52, f32[24,256,128]{2,1,0:T(8,128)} %copy.52), kind=kCustom, calls=%fused_computation.3 | custom fusion | bytes 9437280 | tf_op jit(solution)/shard_map/scatter | solution.py:72
  149.5 4.8 %all-to-all-start.2 = ((f32[8,6,256,128]{3,2,1,0:T(8,128)}), f32[8,6,256,128]{3,2,1,0:T(8,128)}, u32[]{:S(2)}, u32[]{:S(2)}) async-start(f32[8,6,256,128]{3,2,1,0:T(8,128)} %bitcast.104), calls=%async_computation.2 | async-start | bytes 12582912 | tf_op jit(solution)/shard_map/all_to_all | solution.py:74
  155.7 135.1 %all-to-all-done.2 = f32[8,6,256,128]{3,2,1,0:T(8,128)} async-done(((f32[8,6,256,128]{3,2,1,0:T(8,128)}), f32[8,6,256,128]{3,2,1,0:T(8,128)}, u32[]{:S(2)}, u32[]{:S(2)}) %all-to-all-start.2) | async-done | bytes 6291488 | tf_op jit(solution)/shard_map/all_to_all | solution.py:74
  290.8 10.8 %fusion.3 = f32[32,32768]{1,0:T(8,128)} fusion(f32[6,8,256,128]{3,2,1,0:T(8,128)} %bitcast.40, s32[48]{0:T(128)S(1)} %eq.31), kind=kOutput, calls=%fused_computation.10 | convolution fusion | flops 603981312 | bytes 10485952 | tf_op jit(solution)/shard_map/dot_general | solution.py:84
  301.6 0.9 copy.51
  302.6 83.9 %all-reduce.2.cloned.1.call-done = f32[32,32768]{1,0:T(8,128)} async-done(((f32[32,32768]{1,0:T(8,128)}), f32[32,32768]{1,0:T(8,128)}) %all-reduce.2.cloned.1.call-update) | async-done | bytes 4194320 | tf_op jit(solution)/shard_map/psum | solution.py:90
  386.5 4.4 %broadcast_multiply_fusion = f32[32,32768]{1,0:T(8,128)} fusion(f32[32,32768]{1,0:T(8,128)} %all-reduce.2.cloned.1.call-done), kind=kLoop, calls=%fused_computation.19 | loop fusion | flops 1048576 | bytes 8388608 | tf_op jit(solution)/shard_map/div | solution.py:92
  390.9 4.9 %div.83 = f32[8192,128]{1,0:T(8,128)} reshape(f32[32,32768]{1,0:T(8,128)} %broadcast_multiply_fusion) | data formatting | bytes 8388608 | tf_op jit(solution)/shard_map/div | solution.py:92
  (35 shorter events, 4.4 us)
Async XLA Ops:
  7.2 16.6 %copy-start = (bf16[8192,128]{1,0:T(8,128)(2,1)S(1)}, bf16[8192,128]{1,0:T(8,128)(2,1)}, u32[]{:S(2)}) copy-start(bf16[8192,128]{1,0:T(8,128)(2,1)} %param.5) | copy-start | bytes 6291460
  26.5 76.1 %all-to-all-start.1 = ((bf16[8,6,256,128]{3,2,1,0:T(8,128)(2,1)}), bf16[8,6,256,128]{3,2,1,0:T(8,128)(2,1)}, u32[]{:S(2)}, u32[]{:S(2)}) async-start(bf16[8,6,256,128]{3,2,1,0:T(8,128)(2,1)} %bitcast.106), calls=%async_computation.1 | async-start | bytes 6291456 | tf_op jit(solution)/shard_map/all_to_all | solution.py:48
  31.7 25.8 %collective-permute-start = (f32[128,128]{1,0:T(8,128)S(1)}, f32[128,128]{1,0:T(8,128)S(1)}, u32[]{:S(2)}, u32[]{:S(2)}) collective-permute-start(f32[128,128]{1,0:T(8,128)S(1)} %fusion.58), channel_id=1, source_target_pairs={{0,4},{4,0},{8,12},{12,8},{16,20},{20,16},{24,28},{28,24},{1,5},{5... | collective-permute-start | bytes 196616 | tf_op jit(solution)/shard_map/ppermute | solution.py:36
  57.5 25.0 %collective-permute-start.1 = (f32[128,128]{1,0:T(8,128)S(1)}, f32[128,128]{1,0:T(8,128)S(1)}, u32[]{:S(2)}, u32[]{:S(2)}) collective-permute-start(f32[128,128]{1,0:T(8,128)S(1)} %add.140), channel_id=1, source_target_pairs={{0,8},{4,12},{8,0},{12,4},{16,24},{20,28},{24,16},{28,20},{1,9},{5... | collective-permute-start | bytes 196616 | tf_op jit(solution)/shard_map/ppermute | solution.py:36
  82.6 31.7 %collective-permute-start.2 = (f32[128,128]{1,0:T(8,128)S(1)}, f32[128,128]{1,0:T(8,128)S(1)}, u32[]{:S(2)}, u32[]{:S(2)}) collective-permute-start(f32[128,128]{1,0:T(8,128)S(1)} %add.141), channel_id=1, source_target_pairs={{0,16},{4,20},{8,24},{12,28},{16,0},{20,4},{24,8},{28,12},{1,17},{... | collective-permute-start | bytes 196616 | tf_op jit(solution)/shard_map/ppermute | solution.py:36
  122.6 5.2 %copy-start.1 = (f32[3,256,128]{1,2,0:T(8,128)S(1)}, f32[3,256,128]{1,2,0:T(8,128)}, u32[]{:S(2)}) copy-start(f32[3,256,128]{1,2,0:T(8,128)} %multiply_add_fusion.1) | copy-start | bytes 1179652
  149.5 141.3 %all-to-all-start.2 = ((f32[8,6,256,128]{3,2,1,0:T(8,128)}), f32[8,6,256,128]{3,2,1,0:T(8,128)}, u32[]{:S(2)}, u32[]{:S(2)}) async-start(f32[8,6,256,128]{3,2,1,0:T(8,128)} %bitcast.104), calls=%async_computation.2 | async-start | bytes 12582912 | tf_op jit(solution)/shard_map/all_to_all | solution.py:74
  154.2 232.3 %all-reduce.2.cloned.1.call-start = ((), (), s32[]{:S(2)}) async-start(), calls=%async_computation.3 | async-start | bytes 8388608 | tf_op jit(solution)/shard_map/psum | solution.py:90
Sparse Core Ops, SparseCore 0:
  301.8 84.6 all-reduce.1
